TPU v7x, 32 devices: a whole 2x2x4 slice. The times are simulated.
32 devices in a mesh: groups: 2 (over y), az: 4 (over z), rg: 2 (over x), acq: 2 (over core).
Axes of the slice: x: 2, y: 2, z: 4, core: 2. Of those that a mesh axis runs over, the one named last changes fastest.
Arguments:
- image_stack: bfloat16 [2, 64, 32, 4, 256], P(None, ('az', 'acq'), 'groups', 'rg'), parts along dimension 2, may hold values from -12 to 12
- steering: bfloat16 [4, 2, 64, 512], P('rg'), as said below
- wiener_filter: bfloat16 [4, 2, 64, 64], P('rg'), may hold values from -0.5 to 0.5
- range_group: int32 [4], P('rg'), may hold values from 0 to 3, as said below
- lay_list: int32 [32, 4, 32], P(('groups', 'az', 'acq'), 'rg'), parts along dimension 0, may hold values from 0 to 255, as said below
- lay_count: int32 [32, 4], P(('groups', 'az', 'acq'), 'rg'), parts along dimension 0, may hold values from 0 to 32, as said below
Outputs:
- power: bfloat16 [32, 4, 512, 256], P(('groups', 'az', 'acq'), 'rg'), parts along dimension 0
There are 2 independent parts, one for each index of `groups`. A program takes and returns all parts, laid end to end along the dimension named above; an argument that names none is the same for every part. Nothing has to cross between parts.
Inputs may be any that keep to these rules, and one draw needn't show every extreme that they name: `lay_list`: within one block the 32 entries are distinct pixels. The first lay_count entries of a block's list are its layover pixels; some block has 32. `range_group`: range block r belongs to a group from (r // 2) * 2 to (r // 2) * 2 + 1. `steering`: every complex entry has modulus 1 / sqrt(512) up to rounding.
All inputs are finite; a program needn't handle non-finite values.
Results may differ from a plain program's by a relative error of at most 0.0075.
Values may be sent and summed in bfloat16 or wider, within the bound.
No kernel may reach another device: no remote copies, remote signals or barrier semaphores. Data moves between devices by JAX's collectives and lax.ppermute only.
A program may use at most 64 MiB of HBM per device.

v0:
```python
import jax
import jax.numpy as jnp
from jax import lax
from jax.sharding import PartitionSpec as P

K = 64
E = 512
LMAX = 32
GRP_DEV = 2
ITERS = 8
STEP_SIZE = 0.5
SHRINK = 0.25
block_rows = 32


def complex_block(complex_parts):
    real_part = complex_parts[0]
    imag_part = complex_parts[1]
    upper = jnp.concatenate([real_part, -imag_part], axis=1)
    lower = jnp.concatenate([imag_part, real_part], axis=1)
    return jnp.concatenate([upper, lower], axis=0)


def ista_power(lane_data, operator):
    target = lane_data.astype(jnp.float32)
    elevation = operator.shape[1] // 2

    def sweep(sweep_index, estimate):
        rounded = estimate.astype(jnp.bfloat16)
        predicted = jnp.dot(rounded, operator.T, preferred_element_type=jnp.float32)
        misfit = (target - predicted).astype(jnp.bfloat16)
        update = estimate + STEP_SIZE * jnp.dot(
            misfit, operator, preferred_element_type=jnp.float32
        )
        magnitude = update[:, :elevation] ** 2 + update[:, elevation:] ** 2
        factor = jnp.maximum(1.0 - SHRINK * lax.rsqrt(jnp.maximum(magnitude, SHRINK * SHRINK)), 0.0)
        return update * jnp.concatenate([factor, factor], axis=1)

    start = jnp.zeros((lane_data.shape[0], 2 * elevation), jnp.float32)
    estimate = lax.fori_loop(0, ITERS, sweep, start)
    return (estimate[:, :elevation] ** 2 + estimate[:, elevation:] ** 2).astype(jnp.bfloat16)


def pack_order(usable):
    live_flags = usable.astype(jnp.int32)
    live_total = jnp.sum(live_flags)
    before_live = jnp.cumsum(live_flags) - live_flags
    before_empty = jnp.cumsum(1 - live_flags) - (1 - live_flags)
    lane_slot = jnp.where(usable, before_live, live_total + before_empty)
    source = (
        jnp.zeros_like(lane_slot).at[lane_slot].set(jnp.arange(lane_slot.shape[0], dtype=jnp.int32))
    )
    return (lane_slot, source, live_total)


def solve_lanes(lane_data, usable, operator):
    lane_slot, source, live_total = pack_order(usable)
    packed = jnp.take(lane_data, source, axis=0)
    lane_total = lane_data.shape[0]
    elevation = operator.shape[1] // 2

    def one_block(block_turn, result):
        row_block = lax.dynamic_slice_in_dim(packed, block_turn * block_rows, block_rows, 0)
        return lax.dynamic_update_slice_in_dim(
            result, ista_power(row_block, operator), block_turn * block_rows, 0
        )

    turns = (live_total + block_rows - 1) // block_rows
    result = lax.fori_loop(0, turns, one_block, jnp.zeros((lane_total, elevation), jnp.bfloat16))
    return jnp.take(result, lane_slot, axis=0)


def shards(image_stack, steering, wiener_filter, range_group, lay_list, lay_count):
    halves, acq_share, azb_all, range_local, block_pixels = image_stack.shape
    relaid = lax.all_to_all(
        image_stack.reshape(halves, 1, acq_share, azb_all, range_local, block_pixels),
        ("az", "acq"),
        split_axis=3,
        concat_axis=1,
        tiled=True,
    )
    blocks = lay_list.shape[0]
    pixels = relaid.reshape(2 * K, blocks, range_local, block_pixels)
    first_group = lax.axis_index("rg") * GRP_DEV
    operators = []
    wiener_sets = []
    lane_sets = []
    usable_sets = []
    chosen_sets = []
    for column in range(range_local):
        pick_group = jnp.arange(GRP_DEV, dtype=jnp.int32) == range_group[column] - first_group
        steer_parts = jnp.sum(
            jnp.where(pick_group[:, None, None, None], steering, jnp.zeros_like(steering)), axis=0
        )
        filter_parts = jnp.sum(
            jnp.where(
                pick_group[:, None, None, None], wiener_filter, jnp.zeros_like(wiener_filter)
            ),
            axis=0,
        )
        operator = complex_block(steer_parts)
        filter_matrix = complex_block(filter_parts)
        block_data = pixels[:, :, column, :]
        filtered = jnp.einsum(
            "ij,jap->iap", filter_matrix, block_data, preferred_element_type=jnp.float32
        ).astype(jnp.bfloat16)
        beamed = jnp.einsum("ie,iap->aep", operator, filtered, preferred_element_type=jnp.float32)
        wiener_sets.append(beamed[:, :E] ** 2 + beamed[:, E:] ** 2)
        listed = lay_list[:, column, :]
        live_count = lay_count[:, column]
        usable = jnp.arange(LMAX, dtype=jnp.int32)[None, :] < live_count[:, None]
        chosen = (
            (listed[:, :, None] == jnp.arange(block_pixels, dtype=jnp.int32)[None, None, :])
            & usable[:, :, None]
        ).astype(jnp.bfloat16)
        lane_data = jnp.einsum(
            "alp,iap->ali", chosen, block_data, preferred_element_type=jnp.float32
        ).astype(jnp.bfloat16)
        operators.append(operator)
        lane_sets.append(lane_data.reshape(blocks * LMAX, 2 * K))
        usable_sets.append(usable.reshape(blocks * LMAX))
        chosen_sets.append(chosen)
    powers = [
        solve_lanes(lane_sets[column], usable_sets[column], operators[column])
        for column in range(range_local)
    ]
    outputs = []
    for column in range(range_local):
        lay_power = powers[column].reshape(blocks, LMAX, E)
        placed = jnp.einsum(
            "alp,ale->aep", chosen_sets[column], lay_power, preferred_element_type=jnp.float32
        )
        covered = jnp.sum(chosen_sets[column].astype(jnp.float32), axis=1)
        outputs.append(
            jnp.where(covered[:, None, :] > 0.5, placed, wiener_sets[column]).astype(jnp.bfloat16)
        )
    return jnp.stack(outputs, axis=1)


def solution(mesh):
    return jax.shard_map(
        shards,
        mesh=mesh,
        in_specs=(
            P(None, ("az", "acq"), "groups", "rg", None),
            P("rg", None, None, None),
            P("rg", None, None, None),
            P("rg"),
            P(("groups", "az", "acq"), "rg", None),
            P(("groups", "az", "acq"), "rg"),
        ),
        out_specs=P(("groups", "az", "acq"), "rg", None, None),
        check_vma=False,
    )
```

profile of v0, /device:TPU:27, one launch (start us, length us, event | category | flops | bytes accessed | tf_op | source)
XLA Modules:
  0.0 42.8 jit_solution(8267527143187497523)
XLA Ops:
  0.0 1.9 %copy.39 = bf16[2,8,16,2,256]{4,3,1,0,2:T(2,128)(2,1)} copy(bf16[2,8,16,2,256]{4,3,2,1,0:T(2,128)(2,1)} %param.18) | data formatting | bytes 524288 | tf_op args[0]
  1.9 5.4 %all-to-all-start = ((bf16[2,1,8,16,2,256]{5,4,2,0,1,3:T(2,128)(2,1)}), bf16[2,1,8,16,2,256]{5,4,2,0,1,3:T(2,128)(2,1)S(1)}, u32[]{:S(2)}, u32[]{:S(2)}) async-start(bf16[2,1,8,16,2,256]{5,4,2,0,1,3:T(2,128)(2,1)} %bitcast.76), calls=%async_computation | async-start | bytes 524288 | tf_op jit(solution)/shard_map/all_to_all | solution.py:75
  7.3 1.0 %slice_reduce_fusion.1 = (s32[2]{0:T(128)S(1)}, s32[2]{0:T(128)S(1)}) fusion(s32[2,2]{1,0:T(2,128)} %param.23), kind=kLoop, calls=%fused_computation.142 | loop fusion | bytes 32 | tf_op jit(solution)/shard_map/slice | solution.py:110
  8.3 0.7 %convert_reduce_fusion.3 = s32[]{:T(128)} fusion(s32[2]{0:T(128)S(1)} %get-tuple-element.175), kind=kLoop, calls=%fused_computation.139 | loop fusion | flops 191 | bytes 12 | tf_op jit(solution)/shard_map/reduce_sum | solution.py:46
  9.4 0.8 %convert_reduce_fusion.2 = s32[]{:T(128)} fusion(s32[2]{0:T(128)S(1)} %get-tuple-element.176), kind=kLoop, calls=%fused_computation.136 | loop fusion | flops 191 | bytes 12 | tf_op jit(solution)/shard_map/reduce_sum | solution.py:46
  10.6 1.4 %fusion.92 = (s32[64]{0:T(128)S(1)}, s32[64]{0:T(128)S(1)}, s32[64]{0:T(128)S(1)}, s32[64]{0:T(128)S(1)}, s32[64]{0:T(128)S(1)}, /*index=5*/s32[64]{0:T(128)S(1)}) fusion(s32[64,1]{1,0:T(8,128)S(1)} %reduce-window.14, pred[64,1]{1,0:T(8,128)(4,1)S(1)} %lt.160, s32[64,1]{1,0:T(8,128)S(1)} %reduce-window.15, s32[]{:T(128)} %convert_reduce_fusion.3, ...), kind=kLoop, calls=%fused_computation.156 | loop fusion | flops 1152 | bytes 2696 | tf_op jit(solution)/shard_map/reduce-window
  12.0 0.8 %scatter_custom_fusion = s32[64]{0:T(128)S(1)} fusion(s32[64]{0:T(128)S(1)} %get-tuple-element.170, s32[64]{0:T(128)S(1)} %iota.35, s32[]{:T(128)} %constant.130.clone.1), kind=kCustom, calls=%fused_computation.148 | custom fusion | bytes 260 | tf_op jit(solution)/shard_map/scatter | solution.py:51
  12.8 1.3 %fusion.95 = (s32[1]{0:T(128)}, s32[1]{0:T(128)}) fusion(s32[2]{0:T(128)} %param.21), kind=kLoop, calls=%fused_computation.159 | loop fusion | bytes 16 | tf_op jit(solution)/shard_map/slice | solution.py:91
  15.5 1.1 %select_reduce_fusion.1 = (bf16[2,64,512]{2,1,0:T(8,128)(2,1)S(1)}, bf16[2,64,512]{2,1,0:T(8,128)(2,1)S(1)}) fusion(bf16[2,2,64,512]{3,2,1,0:T(8,128)(2,1)} %param.19, pred[2]{0:T(512)(128)(4,1)S(1)} %iota_compare_fusion.5, pred[2]{0:T(512)(128)(4,1)S(1)} %iota_compare_fusion.4), kind=kLoop, calls=%fused_computation.71 | loop fusion | flops 393216 | bytes 524292 | tf_op jit(solution)/shard_map/reduce_sum | solution.py:92
  16.7 0.8 %scatter_custom_fusion.1 = s32[64]{0:T(128)S(1)} fusion(s32[64]{0:T(128)S(1)} %get-tuple-element.230, s32[64]{0:T(128)S(1)} %iota.37, s32[]{:T(128)} %constant.130.clone.1), kind=kCustom, calls=%fused_computation.146 | custom fusion | bytes 260 | tf_op jit(solution)/shard_map/scatter | solution.py:51
  18.6 0.7 %compare_and_fusion = (pred[64]{0:T(512)(128)(4,1)S(1)}, s32[64]{0:T(128)S(1)}) fusion(pred[64]{0:T(512)(128)(4,1)S(1)} %lt.145, s32[64]{0:T(128)S(1)} %get-tuple-element.229, s32[]{:T(128)} %convert_reduce_fusion.2, s32[64]{0:T(128)S(1)} %get-tuple-element.231), kind=kLoop, calls=%fused_computation.132 | loop fusion | flops 768 | bytes 900 | tf_op jit(solution)/shard_map/jit(_take)/and | solution.py:70
  21.1 0.6 %gather_fusion = bf16[64,128]{1,0:T(8,128)(2,1)S(1)} fusion(bf16[64,128]{1,0:T(8,128)(2,1)S(1)} %bitcast.90, s32[1024]{0:T(1024)S(1)} %pad_clamp_fusion.3), kind=kCustom, calls=%fused_computation.clone | custom fusion | bytes 33024 | tf_op jit(solution)/shard_map/jit(_take)/gather | solution.py:58
  21.9 7.7 %while.47 = (s32[]{:T(128)}, bf16[64,512]{1,0:T(8,128)(2,1)S(1)}, s32[]{:T(128)}, bf16[64,128]{1,0:T(8,128)(2,1)S(1)}, bf16[128,1024]{1,0:T(8,128)(2,1)S(1)}, /*...) while((s32[]{:T(128)}, bf16[64,512]{1,0:T(8,128)(2,1)S(1)}, ...), condition=%wide.region_9.11_spmd, body=%wide.region_6.10_spmd.sunk | while | flops 17199112 | bytes 1253674 | solution.py:69
  21.9 3.8 %while.50 = (s32[]{:T(128)}, f32[32,1024]{1,0:T(8,128)S(1)}, bf16[128,1024]{1,0:T(8,128)(2,1)S(1)}, f32[32,128]{1,0:T(8,128)S(1)}, s32[]{:T(128)}, /*index=5*/s32[]{:T(128)}) while((s32[]{:T(128)}, f32[32,1024]{1,0:T(8,128)S(1)}, bf16[128,1024]{1,0:T(8,128)(2,1)S(1)}, f32[32,128]{1,0:T(8,128)S(1)}, s32[]{:T(128)}, ...), condition=%wide.region_8.9_spmd.clone, body=%wide.region_7.8_spmd.clone.sunk | while | flops 17129476 | bytes 1065039 | solution.py:40
  25.8 3.8 %while.50 = (s32[]{:T(128)}, f32[32,1024]{1,0:T(8,128)S(1)}, bf16[128,1024]{1,0:T(8,128)(2,1)S(1)}, f32[32,128]{1,0:T(8,128)S(1)}, s32[]{:T(128)}, /*index=5*/s32[]{:T(128)}) while((s32[]{:T(128)}, f32[32,1024]{1,0:T(8,128)S(1)}, bf16[128,1024]{1,0:T(8,128)(2,1)S(1)}, f32[32,128]{1,0:T(8,128)S(1)}, s32[]{:T(128)}, ...), condition=%wide.region_8.9_spmd.clone, body=%wide.region_7.8_spmd.clone.sunk | while | flops 17129476 | bytes 1065039 | solution.py:40
  29.6 0.6 %gather_fusion.2 = bf16[64,128]{1,0:T(8,128)(2,1)S(1)} fusion(bf16[64,128]{1,0:T(8,128)(2,1)S(1)} %bitcast.89, s32[1024]{0:T(1024)S(1)} %pad_clamp_fusion.1), kind=kCustom, calls=%fused_computation.2.clone | custom fusion | bytes 33024 | tf_op jit(solution)/shard_map/jit(_take)/gather | solution.py:58
  30.3 7.7 %while.49 = (s32[]{:T(128)}, bf16[64,512]{1,0:T(8,128)(2,1)S(1)}, s32[]{:T(128)}, bf16[64,128]{1,0:T(8,128)(2,1)S(1)}, bf16[128,1024]{1,0:T(8,128)(2,1)S(1)}, /*...) while((s32[]{:T(128)}, bf16[64,512]{1,0:T(8,128)(2,1)S(1)}, ...), condition=%wide.region_20.23_spmd, body=%wide.region_17.22_spmd.sunk | while | flops 17199112 | bytes 1253674 | solution.py:69
  30.4 3.8 %while.51 = (s32[]{:T(128)}, f32[32,1024]{1,0:T(8,128)S(1)}, bf16[128,1024]{1,0:T(8,128)(2,1)S(1)}, f32[32,128]{1,0:T(8,128)S(1)}, s32[]{:T(128)}, /*index=5*/s32[]{:T(128)}) while((s32[]{:T(128)}, f32[32,1024]{1,0:T(8,128)S(1)}, bf16[128,1024]{1,0:T(8,128)(2,1)S(1)}, f32[32,128]{1,0:T(8,128)S(1)}, s32[]{:T(128)}, ...), condition=%wide.region_19.21_spmd.clone, body=%wide.region_18.20_spmd.clone.sunk | while | flops 17129476 | bytes 1065039 | solution.py:40
  34.2 3.8 %while.51 = (s32[]{:T(128)}, f32[32,1024]{1,0:T(8,128)S(1)}, bf16[128,1024]{1,0:T(8,128)(2,1)S(1)}, f32[32,128]{1,0:T(8,128)S(1)}, s32[]{:T(128)}, /*index=5*/s32[]{:T(128)}) while((s32[]{:T(128)}, f32[32,1024]{1,0:T(8,128)S(1)}, bf16[128,1024]{1,0:T(8,128)(2,1)S(1)}, f32[32,128]{1,0:T(8,128)S(1)}, s32[]{:T(128)}, ...), condition=%wide.region_19.21_spmd.clone, body=%wide.region_18.20_spmd.clone.sunk | while | flops 17129476 | bytes 1065039 | solution.py:40
  38.1 0.7 %gather_fusion.1 = bf16[64,512]{1,0:T(8,128)(2,1)S(1)} fusion(bf16[64,512]{1,0:T(8,128)(2,1)S(1)} %get-tuple-element.133, s32[1024]{0:T(1024)S(1)} %pad_clamp_fusion.2), kind=kCustom, calls=%fused_computation.1.clone | custom fusion | bytes 131328 | tf_op jit(solution)/shard_map/jit(_take)/gather | solution.py:70
  38.8 0.7 %gather_fusion.3 = bf16[64,512]{1,0:T(8,128)(2,1)S(1)} fusion(bf16[64,512]{1,0:T(8,128)(2,1)S(1)} %get-tuple-element.134, s32[1024]{0:T(1024)S(1)} %pad_clamp_fusion), kind=kCustom, calls=%fused_computation.3.clone | custom fusion | bytes 131328 | tf_op jit(solution)/shard_map/jit(_take)/gather | solution.py:70
  39.6 0.6 %convolution_bitcast_fusion.1 = f32[2,1024,256]{2,1,0:T(8,128)S(1)} fusion(bf16[128,2,2,256]{3,0,1,2:T(8,128)(2,1)S(1)} %bitcast.87, bf16[64,64]{1,0:T(8,128)(2,1)S(1)} %get-tuple-element.236, bf16[64,64]{1,0:T(8,128)(2,1)S(1)} %get-tuple-element.237, bf16[64,64]{1,0:T(8,128)(2,1)S(1)} %get-tuple-element.238, bf16[64,512]{1,0:T(8,128)(2,1)S(1)} %get-tuple-element.232, ...), kind=kOutput, calls=%fused_computation.47 | convolution fusion | flops 152240128 | bytes 2473984 | tf_op jit(solution)/shard_map/ie,iap->aep/dot_general | solution.py:107
  40.7 0.6 %convolution_bitcast_fusion = f32[2,1024,256]{2,1,0:T(8,128)S(1)} fusion(bf16[128,2,2,256]{3,0,1,2:T(8,128)(2,1)S(1)} %bitcast.88, bf16[64,64]{1,0:T(8,128)(2,1)S(1)} %get-tuple-element.224, bf16[64,64]{1,0:T(8,128)(2,1)S(1)} %get-tuple-element.223, bf16[64,64]{1,0:T(8,128)(2,1)S(1)} %get-tuple-element.239, bf16[64,512]{1,0:T(8,128)(2,1)S(1)} %get-tuple-element.220, ...), kind=kOutput, calls=%fused_computation.46 | convolution fusion | flops 152240128 | bytes 2473984 | tf_op jit(solution)/shard_map/ie,iap->aep/dot_general | solution.py:107
  41.8 1.0 %copy.33 = bf16[2,2,512,256]{3,2,1,0:T(8,128)(2,1)} copy(bf16[2,2,512,256]{3,2,0,1:T(8,128)(2,1)S(1)} %pad_maximum_fusion) | data formatting | bytes 2097152 | tf_op jit(solution)/shard_map/stack | solution.py:137
  (164 shorter events, 17.6 us)
Async XLA Ops:
  0.0 17.6 %copy-start.1 = (s32[2,2,32]{2,1,0:T(2,128)S(1)}, s32[2,2,32]{2,1,0:T(2,128)}, u32[]{:S(2)}) copy-start(s32[2,2,32]{2,1,0:T(2,128)} %param.22) | copy-start | bytes 1540
  0.0 18.3 %copy-start = (bf16[2,2,64,64]{3,2,1,0:T(8,128)(2,1)S(1)}, bf16[2,2,64,64]{3,2,1,0:T(8,128)(2,1)}, u32[]{:S(2)}) copy-start(bf16[2,2,64,64]{3,2,1,0:T(8,128)(2,1)} %param.20) | copy-start | bytes 98308
  1.9 18.8 %all-to-all-start = ((bf16[2,1,8,16,2,256]{5,4,2,0,1,3:T(2,128)(2,1)}), bf16[2,1,8,16,2,256]{5,4,2,0,1,3:T(2,128)(2,1)S(1)}, u32[]{:S(2)}, u32[]{:S(2)}) async-start(bf16[2,1,8,16,2,256]{5,4,2,0,1,3:T(2,128)(2,1)} %bitcast.76), calls=%async_computation | async-start | bytes 524288 | tf_op jit(solution)/shard_map/all_to_all | solution.py:75
where the time goes:
time: 43.2 us; the launch traced here: 42.8 us
  matrix products  15 us (35%)
  local copies, waits for them, and re-layouts  9.99 us (23%)
  other arithmetic  8.13 us (19%)
  starting transfers between devices  5.38 us (12%)
  between operations  2.9 us (7%)
  loops' own time  1.45 us (3%)
    dot_general x32, matrix products, sweep(): jnp.dot(misfit, operator, preferred_element_type=jnp.float32)  12.6 us
    all_to_all x1, starting transfers between devices, shards(): lax.all_to_all(image_stack.reshape(halves, 1, acq_share, azb_all, range_l...  5.38 us
    unnamed x5, local copies, waits for them, and re-layouts  1.93 us
    another operation x5, other arithmetic  1.82 us
    scatter x2, local copies, waits for them, and re-layouts, pack_order(): jnp.zeros_like(lane_slot).at[lane_slot]  1.55 us
    reduce_sum x2, other arithmetic, pack_order(): live_total = jnp.sum(live_flags)  1.48 us
    gather x2, local copies, waits for them, and re-layouts, solve_lanes(): return jnp.take(result, lane_slot, axis=0)  1.4 us
    slice x1, local copies, waits for them, and re-layouts, shards(): range_group[column] - first_group  1.34 us
  transfers between devices with their start and end apart: 1, of which 0 were waited for; matrix products, arithmetic and copies ran while one was open for 25% of the time, Pallas kernels for 0%

commit v1 on v0

--- a/solution.py
+++ b/solution.py
@@ -72,13 +72,10 @@
 
 def shards(image_stack, steering, wiener_filter, range_group, lay_list, lay_count):
     halves, acq_share, azb_all, range_local, block_pixels = image_stack.shape
-    relaid = lax.all_to_all(
-        image_stack.reshape(halves, 1, acq_share, azb_all, range_local, block_pixels),
-        ("az", "acq"),
-        split_axis=3,
-        concat_axis=1,
-        tiled=True,
-    )
+    block = image_stack.reshape(halves, 1, acq_share, azb_all, range_local, block_pixels)
+    pieces = jnp.split(block, lax.axis_size(("az", "acq")), axis=3)
+    incoming = lax.all_to_all(jnp.stack(pieces), ("az", "acq"), 0, 0)
+    relaid = jnp.concatenate(incoming, axis=1)
     blocks = lay_list.shape[0]
     pixels = relaid.reshape(2 * K, blocks, range_local, block_pixels)
     first_group = lax.axis_index("rg") * GRP_DEV

time: 43.2 us -> 53 us (1.23)
  local copies, waits for them, and re-layouts: 9.99 us -> 19.3 us
    unnamed x5 -> x11, local copies, waits for them, and re-layouts: 1.93 us -> 9.82 us
    another operation x2 -> x3, local copies, waits for them, and re-layouts: 0.01 us -> 1.41 us  [the longest x1 1.4 us: shards(): incoming = lax.all_to_all(jnp.stack(pieces), ('az', 'acq'), 0, 0)]
  transfers between devices with their start and end apart: 1 -> 1, of which waited for: 0 -> 0; matrix products, arithmetic and copies ran while one was open for 25% -> 20% of each run, Pallas kernels for 0% -> 0%
where the time goes in v1:
time: 53 us; the launch traced here: 52.2 us
  local copies, waits for them, and re-layouts  19.3 us (36%)
  matrix products  15.1 us (28%)
  other arithmetic  8.12 us (15%)
  starting transfers between devices  5.38 us (10%)
  between operations  2.89 us (5%)
  loops' own time  1.45 us (3%)
    dot_general x32, matrix products, sweep(): jnp.dot(misfit, operator, preferred_element_type=jnp.float32)  12.6 us
    unnamed x11, local copies, waits for them, and re-layouts  9.82 us
    all_to_all x1, starting transfers between devices, shards(): incoming = lax.all_to_all(jnp.stack(pieces), ('az', 'acq'), 0, 0)  5.38 us
    another operation x5, other arithmetic  1.82 us
    scatter x2, local copies, waits for them, and re-layouts, pack_order(): jnp.zeros_like(lane_slot).at[lane_slot]  1.55 us
    reduce_sum x2, other arithmetic, pack_order(): live_total = jnp.sum(live_flags)  1.47 us
    gather x2, local copies, waits for them, and re-layouts, solve_lanes(): return jnp.take(result, lane_slot, axis=0)  1.4 us
    another operation x1, local copies, waits for them, and re-layouts, shards(): incoming = lax.all_to_all(jnp.stack(pieces), ('az', 'acq'), 0, 0)  1.4 us
  transfers between devices with their start and end apart: 1, of which 0 were waited for; matrix products, arithmetic and copies ran while one was open for 20% of the time, Pallas kernels for 0%

profile of v1, /device:TPU:27, one launch (start us, length us, event | category | flops | bytes accessed | tf_op | source)
XLA Modules:
  0.0 52.2 jit_solution(9373766455832461404)
XLA Ops:
  0.0 1.4 %fusion.55 = bf16[8,2,1,8,2,2,256]{6,5,4,3,1,2,0:T(2,128)(2,1)} fusion(bf16[2,1,8,16,2,256]{5,4,3,2,0,1:T(2,128)(2,1)} %bitcast.120), kind=kLoop, calls=%fused_computation.108 | loop fusion | bytes 65536
  1.4 1.4 %fusion.54 = bf16[8,2,1,8,2,2,256]{6,5,4,3,1,2,0:T(2,128)(2,1)} fusion(bf16[8,2,1,8,2,2,256]{6,5,4,3,1,2,0:T(2,128)(2,1)} %fusion.55, bf16[2,1,8,16,2,256]{5,4,3,2,0,1:T(2,128)(2,1)} %bitcast.121), kind=kLoop, calls=%fused_computation.106 | loop fusion | bytes 65536
  2.8 1.4 %fusion.53 = bf16[8,2,1,8,2,2,256]{6,5,4,3,1,2,0:T(2,128)(2,1)} fusion(bf16[8,2,1,8,2,2,256]{6,5,4,3,1,2,0:T(2,128)(2,1)} %fusion.54, bf16[2,1,8,16,2,256]{5,4,3,2,0,1:T(2,128)(2,1)} %bitcast.122), kind=kLoop, calls=%fused_computation.104 | loop fusion | bytes 65536
  4.2 1.4 %fusion.52 = bf16[8,2,1,8,2,2,256]{6,5,4,3,1,2,0:T(2,128)(2,1)} fusion(bf16[8,2,1,8,2,2,256]{6,5,4,3,1,2,0:T(2,128)(2,1)} %fusion.53, bf16[2,1,8,16,2,256]{5,4,3,2,0,1:T(2,128)(2,1)} %bitcast.123), kind=kLoop, calls=%fused_computation.102 | loop fusion | bytes 65536
  5.6 1.4 %fusion.51 = bf16[8,2,1,8,2,2,256]{6,5,4,3,1,2,0:T(2,128)(2,1)} fusion(bf16[8,2,1,8,2,2,256]{6,5,4,3,1,2,0:T(2,128)(2,1)} %fusion.52, bf16[2,1,8,16,2,256]{5,4,3,2,0,1:T(2,128)(2,1)} %bitcast.124), kind=kLoop, calls=%fused_computation.100 | loop fusion | bytes 65536
  7.0 1.4 %fusion.50 = bf16[8,2,1,8,2,2,256]{6,5,4,3,1,2,0:T(2,128)(2,1)} fusion(bf16[8,2,1,8,2,2,256]{6,5,4,3,1,2,0:T(2,128)(2,1)} %fusion.51, bf16[2,1,8,16,2,256]{5,4,3,2,0,1:T(2,128)(2,1)} %bitcast.125), kind=kLoop, calls=%fused_computation.98 | loop fusion | bytes 65536
  8.4 1.4 %fusion.49 = bf16[8,2,1,8,2,2,256]{6,5,4,3,1,2,0:T(2,128)(2,1)} fusion(bf16[8,2,1,8,2,2,256]{6,5,4,3,1,2,0:T(2,128)(2,1)} %fusion.50, bf16[2,1,8,16,2,256]{5,4,3,2,0,1:T(2,128)(2,1)} %bitcast.126), kind=kLoop, calls=%fused_computation.96 | loop fusion | bytes 65536
  9.8 1.4 %fusion.48 = bf16[8,2,1,8,2,2,256]{6,5,4,3,1,2,0:T(2,128)(2,1)} fusion(bf16[8,2,1,8,2,2,256]{6,5,4,3,1,2,0:T(2,128)(2,1)} %fusion.49, bf16[2,1,8,16,2,256]{5,4,3,2,0,1:T(2,128)(2,1)} %bitcast.127), kind=kLoop, calls=%fused_computation.94 | loop fusion | bytes 65536 | tf_op jit(solution)/shard_map/stack | solution.py:77
  11.2 5.4 %all-to-all-start = ((bf16[8,2,1,8,2,2,256]{6,5,4,3,1,2,0:T(2,128)(2,1)}), bf16[8,2,1,8,2,2,256]{6,5,4,3,1,2,0:T(2,128)(2,1)S(1)}, u32[]{:S(2)}, u32[]{:S(2)}) async-start(bf16[8,2,1,8,2,2,256]{6,5,4,3,1,2,0:T(2,128)(2,1)} %fusion.48), calls=%async_computation | async-start | bytes 524288 | tf_op jit(solution)/shard_map/all_to_all | solution.py:77
  16.6 1.0 %slice_reduce_fusion.1 = (s32[2]{0:T(128)S(1)}, s32[2]{0:T(128)S(1)}) fusion(s32[2,2]{1,0:T(2,128)} %param.23), kind=kLoop, calls=%fused_computation.157 | loop fusion | bytes 32 | tf_op jit(solution)/shard_map/slice | solution.py:107
  18.0 0.8 %convert_reduce_fusion.2 = s32[]{:T(128)} fusion(s32[2]{0:T(128)S(1)} %get-tuple-element.176), kind=kLoop, calls=%fused_computation.151 | loop fusion | flops 191 | bytes 12 | tf_op jit(solution)/shard_map/reduce_sum | solution.py:46
  19.9 1.4 %fusion.100 = (s32[64]{0:T(128)S(1)}, s32[64]{0:T(128)S(1)}, s32[64]{0:T(128)S(1)}, s32[64]{0:T(128)S(1)}, s32[64]{0:T(128)S(1)}, /*index=5*/s32[64]{0:T(128)S(1)}) fusion(s32[64,1]{1,0:T(8,128)S(1)} %reduce-window.14, pred[64,1]{1,0:T(8,128)(4,1)S(1)} %lt.160, s32[64,1]{1,0:T(8,128)S(1)} %reduce-window.15, s32[]{:T(128)} %convert_reduce_fusion.3, ...), kind=kLoop, calls=%fused_computation.171 | loop fusion | flops 1152 | bytes 2696 | tf_op jit(solution)/shard_map/reduce-window
  21.3 0.8 %scatter_custom_fusion = s32[64]{0:T(128)S(1)} fusion(s32[64]{0:T(128)S(1)} %get-tuple-element.170, s32[64]{0:T(128)S(1)} %iota.35, s32[]{:T(128)} %constant.130.clone.1), kind=kCustom, calls=%fused_computation.163 | custom fusion | bytes 260 | tf_op jit(solution)/shard_map/scatter | solution.py:51
  22.1 1.3 %fusion.103 = (s32[1]{0:T(128)}, s32[1]{0:T(128)}) fusion(s32[2]{0:T(128)} %param.21), kind=kLoop, calls=%fused_computation.174 | loop fusion | bytes 16 | tf_op jit(solution)/shard_map/slice | solution.py:88
  24.8 1.1 %select_reduce_fusion.1 = (bf16[2,64,512]{2,1,0:T(8,128)(2,1)S(1)}, bf16[2,64,512]{2,1,0:T(8,128)(2,1)S(1)}) fusion(bf16[2,2,64,512]{3,2,1,0:T(8,128)(2,1)} %param.19, pred[2]{0:T(512)(128)(4,1)S(1)} %iota_compare_fusion.5, pred[2]{0:T(512)(128)(4,1)S(1)} %iota_compare_fusion.4), kind=kLoop, calls=%fused_computation.70 | loop fusion | flops 393216 | bytes 524292 | tf_op jit(solution)/shard_map/reduce_sum | solution.py:89
  26.0 0.8 %scatter_custom_fusion.1 = s32[64]{0:T(128)S(1)} fusion(s32[64]{0:T(128)S(1)} %get-tuple-element.230, s32[64]{0:T(128)S(1)} %iota.37, s32[]{:T(128)} %constant.130.clone.1), kind=kCustom, calls=%fused_computation.161 | custom fusion | bytes 260 | tf_op jit(solution)/shard_map/scatter | solution.py:51
  31.2 7.7 %while.47 = (s32[]{:T(128)}, bf16[64,512]{1,0:T(8,128)(2,1)S(1)}, s32[]{:T(128)}, bf16[64,128]{1,0:T(8,128)(2,1)S(1)}, bf16[128,1024]{1,0:T(8,128)(2,1)S(1)}, /*...) while((s32[]{:T(128)}, bf16[64,512]{1,0:T(8,128)(2,1)S(1)}, ...), condition=%wide.region_9.11_spmd, body=%wide.region_6.10_spmd.sunk | while | flops 17199112 | bytes 1253674 | solution.py:69
  31.2 3.8 %while.50 = (s32[]{:T(128)}, f32[32,1024]{1,0:T(8,128)S(1)}, bf16[128,1024]{1,0:T(8,128)(2,1)S(1)}, f32[32,128]{1,0:T(8,128)S(1)}, s32[]{:T(128)}, /*index=5*/s32[]{:T(128)}) while((s32[]{:T(128)}, f32[32,1024]{1,0:T(8,128)S(1)}, bf16[128,1024]{1,0:T(8,128)(2,1)S(1)}, f32[32,128]{1,0:T(8,128)S(1)}, s32[]{:T(128)}, ...), condition=%wide.region_8.9_spmd.clone, body=%wide.region_7.8_spmd.clone.sunk | while | flops 17129476 | bytes 1065039 | solution.py:40
  35.1 3.8 %while.50 = (s32[]{:T(128)}, f32[32,1024]{1,0:T(8,128)S(1)}, bf16[128,1024]{1,0:T(8,128)(2,1)S(1)}, f32[32,128]{1,0:T(8,128)S(1)}, s32[]{:T(128)}, /*index=5*/s32[]{:T(128)}) while((s32[]{:T(128)}, f32[32,1024]{1,0:T(8,128)S(1)}, bf16[128,1024]{1,0:T(8,128)(2,1)S(1)}, f32[32,128]{1,0:T(8,128)S(1)}, s32[]{:T(128)}, ...), condition=%wide.region_8.9_spmd.clone, body=%wide.region_7.8_spmd.clone.sunk | while | flops 17129476 | bytes 1065039 | solution.py:40
  39.6 7.7 %while.49 = (s32[]{:T(128)}, bf16[64,512]{1,0:T(8,128)(2,1)S(1)}, s32[]{:T(128)}, bf16[64,128]{1,0:T(8,128)(2,1)S(1)}, bf16[128,1024]{1,0:T(8,128)(2,1)S(1)}, /*...) while((s32[]{:T(128)}, bf16[64,512]{1,0:T(8,128)(2,1)S(1)}, ...), condition=%wide.region_20.23_spmd, body=%wide.region_17.22_spmd.sunk | while | flops 17199112 | bytes 1253674 | solution.py:69
  39.7 3.8 %while.51 = (s32[]{:T(128)}, f32[32,1024]{1,0:T(8,128)S(1)}, bf16[128,1024]{1,0:T(8,128)(2,1)S(1)}, f32[32,128]{1,0:T(8,128)S(1)}, s32[]{:T(128)}, /*index=5*/s32[]{:T(128)}) while((s32[]{:T(128)}, f32[32,1024]{1,0:T(8,128)S(1)}, bf16[128,1024]{1,0:T(8,128)(2,1)S(1)}, f32[32,128]{1,0:T(8,128)S(1)}, s32[]{:T(128)}, ...), condition=%wide.region_19.21_spmd.clone, body=%wide.region_18.20_spmd.clone.sunk | while | flops 17129476 | bytes 1065039 | solution.py:40
  43.5 3.8 %while.51 = (s32[]{:T(128)}, f32[32,1024]{1,0:T(8,128)S(1)}, bf16[128,1024]{1,0:T(8,128)(2,1)S(1)}, f32[32,128]{1,0:T(8,128)S(1)}, s32[]{:T(128)}, /*index=5*/s32[]{:T(128)}) while((s32[]{:T(128)}, f32[32,1024]{1,0:T(8,128)S(1)}, bf16[128,1024]{1,0:T(8,128)(2,1)S(1)}, f32[32,128]{1,0:T(8,128)S(1)}, s32[]{:T(128)}, ...), condition=%wide.region_19.21_spmd.clone, body=%wide.region_18.20_spmd.clone.sunk | while | flops 17129476 | bytes 1065039 | solution.py:40
  47.3 0.7 %gather_fusion.1 = bf16[64,512]{1,0:T(8,128)(2,1)S(1)} fusion(bf16[64,512]{1,0:T(8,128)(2,1)S(1)} %get-tuple-element.133, s32[1024]{0:T(1024)S(1)} %pad_clamp_fusion.2), kind=kCustom, calls=%fused_computation.1.clone | custom fusion | bytes 131328 | tf_op jit(solution)/shard_map/jit(_take)/gather | solution.py:70
  51.1 1.0 %copy.22 = bf16[2,2,512,256]{3,2,1,0:T(8,128)(2,1)} copy(bf16[2,2,512,256]{3,2,0,1:T(8,128)(2,1)S(1)} %pad_maximum_fusion) | data formatting | bytes 2097152 | tf_op jit(solution)/shard_map/stack | solution.py:134
  (171 shorter events, 22.3 us)
Async XLA Ops:
  0.0 26.9 %copy-start.1 = (s32[2,2,32]{2,1,0:T(2,128)S(1)}, s32[2,2,32]{2,1,0:T(2,128)}, u32[]{:S(2)}) copy-start(s32[2,2,32]{2,1,0:T(2,128)} %param.22) | copy-start | bytes 1540
  0.0 27.5 %copy-start = (bf16[2,2,64,64]{3,2,1,0:T(8,128)(2,1)S(1)}, bf16[2,2,64,64]{3,2,1,0:T(8,128)(2,1)}, u32[]{:S(2)}) copy-start(bf16[2,2,64,64]{3,2,1,0:T(8,128)(2,1)} %param.20) | copy-start | bytes 98308
  11.2 18.8 %all-to-all-start = ((bf16[8,2,1,8,2,2,256]{6,5,4,3,1,2,0:T(2,128)(2,1)}), bf16[8,2,1,8,2,2,256]{6,5,4,3,1,2,0:T(2,128)(2,1)S(1)}, u32[]{:S(2)}, u32[]{:S(2)}) async-start(bf16[8,2,1,8,2,2,256]{6,5,4,3,1,2,0:T(2,128)(2,1)} %fusion.48), calls=%async_computation | async-start | bytes 524288 | tf_op jit(solution)/shard_map/all_to_all | solution.py:77
